TPU v7x, 32 devices: a whole 2x2x4 slice. The times are simulated.
32 devices in a mesh: b: 4 (over z), a: 8 (over y, x, core).
Axes of the slice: x: 2, y: 2, z: 4, core: 2. Of those that a mesh axis runs over, the one named last changes fastest.
Arguments:
- u: float32 [256, 256, 256], P(None, 'a', 'b')
- g: float32 [136, 256, 256], P('a', 'b')
Outputs:
- output: float32 [256, 256, 256], P(None, 'a', 'b')
All inputs are finite; a program needn't handle non-finite values.
Results may differ from a plain program's by a relative error of at most 0.001.
Values are sent between devices in bfloat16 or wider.
A program may use at most 1 GiB of HBM per device.

v0:
```python
import math
import functools
import jax
import jax.numpy as jnp
from jax import lax
from jax.sharding import PartitionSpec as P

HI = lax.Precision.HIGHEST


def _trig(n, rows, cols):
    r = jnp.arange(rows, dtype=jnp.int32)[:, None]
    c = jnp.arange(cols, dtype=jnp.int32)[None, :]
    ang = ((r * c) % n).astype(jnp.float32) * (2.0 * math.pi / n)
    return jnp.cos(ang), jnp.sin(ang)


def _xtables(n, kx):
    cx, sx = _trig(n, kx, n)
    k = jnp.arange(kx)
    keep = (k <= n // 2).astype(jnp.float32)
    wgt = jnp.where((k == 0) | (k == n // 2), 1.0, 2.0) * keep / n
    return cx * keep[:, None], -sx * keep[:, None], (cx * wgt[:, None]).T, (sx * wgt[:, None]).T


def _mm(p, q):
    return jnp.dot(p, q, precision=HI, preferred_element_type=jnp.float32)


def _line(x, c, s, form, sign):
    e = functools.partial(jnp.einsum, form, precision=HI, preferred_element_type=jnp.float32)
    return jnp.stack([e(x[0], c) + sign * e(x[1], s), e(x[1], c) - sign * e(x[0], s)])


def solution(mesh):
    na = mesh.shape["a"]

    def local(u, g):
        n, ya, zb = u.shape
        kx = g.shape[0] * na
        c1, s1, ar, ai = _xtables(n, kx)
        c, s = _trig(n, n, n)
        ci, si = c / n, s / n
        u2 = u.reshape(n, ya * zb)
        x = jnp.stack([_mm(c1, u2), _mm(s1, u2)]).reshape(2, kx, ya, zb)
        x = lax.all_to_all(x, "a", 1, 2, tiled=True)
        x = _line(x, c, s, "xyz,yk->xkz", 1.0)
        x = lax.all_to_all(x, "b", 2, 3, tiled=True)
        x = _line(x, c, s, "xyz,zk->xyk", 1.0) * g[None]
        x = _line(x, ci, si, "xyz,zk->xyk", -1.0)
        x = lax.all_to_all(x, "b", 3, 2, tiled=True)
        x = _line(x, ci, si, "xyz,yk->xkz", -1.0)
        x = lax.all_to_all(x, "a", 2, 1, tiled=True)
        w = _mm(ar, x[0].reshape(kx, ya * zb)) - _mm(ai, x[1].reshape(kx, ya * zb))
        return w.reshape(n, ya, zb)

    return jax.shard_map(local, mesh=mesh, in_specs=(P(None, "a", "b"), P("a", "b", None)), out_specs=P(None, "a", "b"), check_vma=False)
```

profile of v0, /device:TPU:0, one launch (start us, length us, event | category | flops | bytes accessed | tf_op | source)
XLA Modules:
  0.0 410.2 jit_solution(531636858215304392)
XLA Ops:
  1.6 2.3 fusion.4
  3.9 2.3 fusion.7
  6.3 2.3 pad_maximum_fusion
  8.6 6.0 %copy.42 = f32[2,136,32,64]{3,2,0,1:T(8,128)} copy(f32[2,136,32,64]{1,3,2,0:T(8,128)} %pad_maximum_fusion) | data formatting | bytes 4456448 | tf_op jit(solution)/shard_map/stack | solution.py:45
  14.6 7.4 %reshape.171 = f32[8,1,69632]{2,1,0:T(1,128)} reshape(f32[136,2,32,64]{3,2,1,0:T(8,128)} %bitcast.158) | data formatting | bytes 4456448
  22.0 33.2 %all_to_all.60 = f32[8,1,69632]{2,1,0:T(1,128)} all-to-all(f32[8,1,69632]{2,1,0:T(1,128)} %reshape.171), channel_id=1, replica_groups=mesh['b'=4,'a'=8] {'a'}, dimensions={0} | all-to-all | bytes 4456448 | tf_op jit(solution)/shard_map/all_to_all | solution.py:46
  55.7 9.0 %reduce = f32[8,69632]{1,0:T(8,128)} reduce(f32[8,1,69632]{2,1,0:T(1,128)} %all_to_all.60, f32[]{:T(128)} %broadcast.303), dimensions={1}, to_apply=%all_to_all.44.reduce_sub_computation | reduce | bytes 4456452 | tf_op jit(solution)/shard_map/all_to_all | solution.py:46
  64.7 5.4 %reshape.172 = f32[136,2,32,64]{3,2,1,0:T(8,128)} reshape(f32[8,69632]{1,0:T(8,128)} %reduce) | data formatting | bytes 4456448
  70.2 2.8 copy.43
  73.0 2.0 fusion.200
  75.0 1.6 copy.46
  76.6 2.2 copy.47
  78.8 2.0 fusion.94
  80.8 3.0 fusion.81
  83.9 1.6 copy.44
  85.5 2.0 copy.45
  87.4 2.1 fusion.83
  89.5 2.1 fusion.92
  91.9 1.6 pad_maximum_fusion.1
  93.5 7.1 %copy.50 = f32[2,17,256,64]{3,0,1,2:T(2,128)} copy(f32[2,17,256,64]{2,3,1,0:T(8,128)} %pad_maximum_fusion.1) | data formatting | bytes 4456448 | tf_op jit(solution)/shard_map/stack | solution.py:32
  100.5 7.1 %reshape.173 = f32[4,1,139264]{2,1,0:T(1,128)} reshape(f32[256,17,2,64]{3,2,1,0:T(2,128)} %bitcast.160) | data formatting | bytes 4456448
  107.7 56.5 %all_to_all.61 = f32[4,1,139264]{2,1,0:T(1,128)} all-to-all(f32[4,1,139264]{2,1,0:T(1,128)} %reshape.173), channel_id=1, replica_groups=mesh['b'=4,'a'=8] {'b'}, dimensions={0} | all-to-all | bytes 4456448 | tf_op jit(solution)/shard_map/all_to_all | solution.py:48
  164.2 9.1 %reduce.1 = f32[4,139264]{1,0:T(4,128)} reduce(f32[4,1,139264]{2,1,0:T(1,128)} %all_to_all.61, f32[]{:T(128)} %broadcast.303), dimensions={1}, to_apply=%all_to_all.47.reduce_sub_computation | reduce | bytes 4456452 | tf_op jit(solution)/shard_map/all_to_all | solution.py:48
  173.3 7.2 %reshape.174 = f32[256,17,2,64]{3,2,1,0:T(2,128)} reshape(f32[4,139264]{1,0:T(4,128)} %reduce.1) | data formatting | bytes 4456448
  180.5 5.1 %copy.62 = f32[2,17,4,64,64]{4,2,3,1,0:T(4,128)S(1)} copy(f32[2,17,4,64,64]{4,0,1,3,2:T(2,128)} %bitcast.161) | data formatting | bytes 4456448 | tf_op jit(solution)/shard_map/all_to_all | solution.py:48
  185.6 2.5 fusion.199
  188.1 2.5 squeeze.34
  190.7 3.0 fusion.25
  193.7 2.7 squeeze.35
  196.4 2.0 fusion.23
  198.5 2.1 fusion.13
  200.6 2.1 fusion.12
  203.0 2.0 convolution_multiply_fusion.1
  205.0 2.0 convolution_multiply_fusion
  207.0 2.4 fusion.11
  209.5 2.0 fusion.10
  211.5 1.6 pad_maximum_fusion.2
  213.1 7.1 %copy.52 = f32[2,17,64,256]{2,0,1,3:T(2,128)} copy(f32[2,17,64,256]{3,2,1,0:T(8,128)} %pad_maximum_fusion.2) | data formatting | bytes 4456448 | tf_op jit(solution)/shard_map/stack | solution.py:32
  220.2 7.1 %reshape.175 = f32[4,1,139264]{2,1,0:T(1,128)} reshape(f32[256,17,2,64]{3,2,1,0:T(2,128)} %bitcast.162) | data formatting | bytes 4456448
  227.3 55.0 %all_to_all.62 = f32[4,1,139264]{2,1,0:T(1,128)} all-to-all(f32[4,1,139264]{2,1,0:T(1,128)} %reshape.175), channel_id=1, replica_groups=mesh['b'=4,'a'=8] {'b'}, dimensions={0} | all-to-all | bytes 4456448 | tf_op jit(solution)/shard_map/all_to_all | solution.py:51
  282.3 9.1 %reduce.2 = f32[4,139264]{1,0:T(4,128)} reduce(f32[4,1,139264]{2,1,0:T(1,128)} %all_to_all.62, f32[]{:T(128)} %broadcast.303), dimensions={1}, to_apply=%all_to_all.50.reduce_sub_computation | reduce | bytes 4456452 | tf_op jit(solution)/shard_map/all_to_all | solution.py:51
  291.5 7.2 %reshape.176 = f32[256,17,2,64]{3,2,1,0:T(2,128)} reshape(f32[4,139264]{1,0:T(4,128)} %reduce.2) | data formatting | bytes 4456448
  298.6 5.1 %copy.61 = f32[2,17,64,4,64]{2,3,4,1,0:T(4,128)S(1)} copy(f32[2,17,64,4,64]{2,0,1,4,3:T(2,128)} %bitcast.163) | data formatting | bytes 4456448 | tf_op jit(solution)/shard_map/all_to_all | solution.py:51
  303.8 2.5 fusion.198
  306.3 2.7 squeeze.39
  309.0 3.0 fusion.31
  312.1 2.0 fusion.39
  314.1 2.6 squeeze.38
  316.7 2.1 fusion.37
  318.7 2.1 fusion.33
  322.7 7.1 %copy.54 = f32[2,17,256,64]{3,0,1,2:T(2,128)} copy(f32[2,17,256,64]{2,3,1,0:T(8,128)} %pad_maximum_fusion.3) | data formatting | bytes 4456448 | tf_op jit(solution)/shard_map/stack | solution.py:32
  329.8 8.4 %reshape.177 = f32[8,1,69632]{2,1,0:T(1,128)} reshape(f32[256,17,2,64]{3,2,1,0:T(2,128)} %bitcast.164) | data formatting | bytes 4456448
  338.1 4.6 %all-to-all-start.3 = ((f32[8,1,69632]{2,1,0:T(1,128)}), f32[8,1,69632]{2,1,0:T(1,128)}, u32[]{:S(2)}, u32[]{:S(2)}) async-start(f32[8,1,69632]{2,1,0:T(1,128)} %reshape.177), calls=%async_computation.3 | async-start | bytes 4456448 | tf_op jit(solution)/shard_map/all_to_all | solution.py:53
  342.7 27.9 %all-to-all-done.3 = f32[8,1,69632]{2,1,0:T(1,128)} async-done(((f32[8,1,69632]{2,1,0:T(1,128)}), f32[8,1,69632]{2,1,0:T(1,128)}, u32[]{:S(2)}, u32[]{:S(2)}) %all-to-all-start.3) | async-done | bytes 2228256 | tf_op jit(solution)/shard_map/all_to_all | solution.py:53
  370.6 9.0 %reduce.3 = f32[8,69632]{1,0:T(8,128)} reduce(f32[8,1,69632]{2,1,0:T(1,128)} %all-to-all-done.3, f32[]{:T(128)} %broadcast.303), dimensions={1}, to_apply=%all_to_all.53.reduce_sub_computation | reduce | bytes 4456452 | tf_op jit(solution)/shard_map/all_to_all | solution.py:53
  379.6 6.9 %reshape.178 = f32[256,17,2,64]{3,2,1,0:T(2,128)} reshape(f32[8,69632]{1,0:T(8,128)} %reduce.3) | data formatting | bytes 4456448
  386.5 2.8 copy.55
  389.4 2.2 fusion.197
  393.1 2.1 reshape_squeeze.6
  395.3 3.2 copy.57
  398.5 2.4 reshape_squeeze.7
  400.9 2.3 fusion.59
  403.3 3.8 convolution_subtract_fusion
  407.0 2.9 copy.58
  (23 shorter events, 6.3 us)
Async XLA Ops:
  0.0 1.6 copy-start
  80.8 3.0 copy-start.2
  89.5 2.1 copy-start.3
  196.4 2.0 copy-start.5
  200.5 2.1 copy-start.6
  318.7 2.1 copy-start.4
  338.1 32.5 %all-to-all-start.3 = ((f32[8,1,69632]{2,1,0:T(1,128)}), f32[8,1,69632]{2,1,0:T(1,128)}, u32[]{:S(2)}, u32[]{:S(2)}) async-start(f32[8,1,69632]{2,1,0:T(1,128)} %reshape.177), calls=%async_computation.3 | async-start | bytes 4456448 | tf_op jit(solution)/shard_map/all_to_all | solution.py:53
  403.3 6.7 %copy-start.1 = (f32[256,32,64]{0,2,1:T(8,128)S(1)}, f32[256,32,64]{0,2,1:T(8,128)}, u32[]{:S(2)}) copy-start(f32[256,32,64]{0,2,1:T(8,128)} %param.2) | copy-start | bytes 6291460
where the time goes:
time: 417 us; the launch traced here: 410 us
  blocking collectives  145 us (35%)
  local copies, waits for them, and re-layouts  141 us (34%)
  matrix products  46.9 us (11%)
  other arithmetic  44.3 us (11%)
  waiting for transfers between devices  27.9 us (7%)
  starting transfers between devices  4.56 us (1%)
    unnamed x22, local copies, waits for them, and re-layouts  58.2 us
    all_to_all x1, blocking collectives, local(): x = lax.all_to_all(x, 'b', 2, 3, tiled=True)  56.5 us
    all_to_all x1, blocking collectives, local(): x = lax.all_to_all(x, 'b', 3, 2, tiled=True)  55 us
    all_to_all x1, blocking collectives, local(): x = lax.all_to_all(x, 'a', 1, 2, tiled=True)  33.2 us
    all_to_all x1, waiting for transfers between devices, local(): x = lax.all_to_all(x, 'a', 2, 1, tiled=True)  27.9 us
    another operation x3, local copies, waits for them, and re-layouts, _line(): jnp.stack([e(x[0], c) + sign * e(x[1], s), e(x[1], c) - sign * e(x[0], s)])  21.2 us
    unnamed x8, matrix products  18.4 us
    dot_general x4, matrix products, _mm(): return jnp.dot(p, q, precision=HI, preferred_element_type=jnp.float32)  10.8 us
  transfers between devices with their start and end apart: 1, of which 1 were waited for; matrix products, arithmetic and copies ran while one was open for 0% of the time, Pallas kernels for 0%

commit v1 on v0

v1 whole, which is shorter than its diff:
```python
import functools
import math
import numpy as np
import jax
import jax.numpy as jnp
from jax import lax
from jax.experimental import pallas as pl
from jax.experimental.pallas import tpu as pltpu
from jax.sharding import PartitionSpec as P

HI = lax.Precision.HIGHEST
MESH = pl.DeviceIdType.MESH
F32 = jnp.float32
KC = 2


def _trig(n, rows, cols):
    r = np.arange(rows)[:, None]
    c = np.arange(cols)[None, :]
    ang = ((r * c) % n).astype(np.float32) * np.float32(2.0 * math.pi / n)
    ang = ang.astype(np.float64)
    return np.cos(ang).astype(np.float32), np.sin(ang).astype(np.float32)


def _tables(n, kx, nb):
    cx, sx = _trig(n, kx, n)
    k = np.arange(kx)
    keep = (k <= n // 2).astype(np.float32)[:, None]
    wgt = np.where((k == 0) | (k == n // 2), 1.0, 2.0).astype(np.float32)[:, None] * keep / np.float32(n)
    tx = np.concatenate([cx * keep, -sx * keep], axis=0)
    txi = np.concatenate([cx * wgt, -sx * wgt], axis=0)
    c, s = _trig(n, n, n)
    ty = np.concatenate([c, s], axis=0)
    zb = n // nb
    rows = []
    for b in range(nb):
        cb, sb = c[b * zb:(b + 1) * zb], s[b * zb:(b + 1) * zb]
        rows += [np.concatenate([cb, -sb], axis=1), np.concatenate([sb, cb], axis=1)]
    tz = np.concatenate(rows, axis=0)
    return [np.ascontiguousarray(t, dtype=np.float32) for t in (tx, txi, ty, tz)]


def _dot(p, q, dims=((1,), (0,))):
    return lax.dot_general(p, q, (dims, ((), ())), precision=HI, preferred_element_type=F32)


def _kernel(n, na, nb, kl, u_hbm, g_hbm, tx_hbm, txi_hbm, ty_hbm, tz_hbm, w_hbm,
            u, g, tx, txi, ty, tz, xs, ai, yf, bi, bo, vi, iy, ao, w,
            lsem, usem, wsem, ssem, ra, rb, rbo, rao):
    a, b = lax.axis_index("a"), lax.axis_index("b")
    ya, zb = n // na, n // nb
    kx = na * kl
    rows = 4 * zb
    nj = ya * zb // rows
    full, rest = kl // KC, kl % KC

    def local(src, dst, sem):
        return pltpu.make_async_copy(src, dst, sem)

    load_u = [local(u_hbm.at[pl.ds(j * rows, rows)], u.at[pl.ds(j * rows, rows)], usem.at[j]) for j in range(nj)]
    loads = [local(s, d, lsem.at[i]) for i, (s, d) in enumerate(
        [(tx_hbm, tx), (ty_hbm, ty), (tz_hbm, tz), (g_hbm, g), (txi_hbm, txi)])]
    loads[0].start()
    for cp in load_u:
        cp.start()
    for cp in loads[1:]:
        cp.start()

    bar = pltpu.get_barrier_semaphore()
    for d in range(1, na):
        pl.semaphore_signal(bar, inc=1, device_id=(b, lax.rem(a + d, na)), device_id_type=MESH)
    for d in range(1, nb):
        pl.semaphore_signal(bar, inc=1, device_id=(lax.rem(b + d, nb), a), device_id_type=MESH)
    pl.semaphore_wait(bar, na + nb - 2)

    def lanes(shape):
        return lax.broadcasted_iota(jnp.int32, shape, 1) < zb

    xs2 = xs.reshape(kx * ya, 2 * zb)
    ao2 = ao.reshape(kx * ya, 2 * zb)

    loads[0].wait()

    def xfwd(j, _):
        local(u_hbm.at[pl.ds(j * rows, rows)], u.at[pl.ds(j * rows, rows)], usem.at[j]).wait()
        r = _dot(tx[...], u[pl.ds(pl.multiple_of(j * rows, rows), rows), :], ((1,), (1,)))
        lo = lanes((kx, 2 * zb))
        for h in range(2):
            re = r[:kx, 2 * zb * h:2 * zb * (h + 1)]
            im = r[kx:, 2 * zb * h:2 * zb * (h + 1)]
            y = 4 * j + 2 * h
            xs2[pl.ds(y, kx, stride=ya), :] = jnp.where(lo, re, pltpu.roll(im, zb, 1))
            xs2[pl.ds(y + 1, kx, stride=ya), :] = jnp.where(lo, pltpu.roll(re, zb, 1), im)
        return 0

    lax.fori_loop(0, nj, xfwd, 0)

    def chunks(step):
        def body(c, _):
            step(c, c * KC, KC)
            return 0
        lax.fori_loop(0, full, body, 0)
        if rest:
            step(full, full * KC, rest)

    def send_a(c, k, kc):
        for d in range(1, na):
            t = lax.rem(a + d, na)
            pltpu.make_async_remote_copy(
                xs.at[pl.ds(t * kl + k, kc)], ai.at[pl.ds(k, kc), pl.ds(a * ya, ya)],
                ssem.at[0], ra.at[c], device_id=(b, t), device_id_type=MESH).start()
        local(xs.at[pl.ds(a * kl + k, kc)], ai.at[pl.ds(k, kc), pl.ds(a * ya, ya)], ra.at[c]).start()

    chunks(send_a)
    loads[1].wait()

    def ydft(src, dst, k, kc, scale, sign):
        x = jnp.concatenate([src[k + i] for i in range(kc)], axis=1)
        if scale is not None:
            x = x * scale
        r = _dot(ty[...], x)
        lo = lanes((n, 2 * zb))
        for i in range(kc):
            p = r[:n, 2 * zb * i:2 * zb * (i + 1)]
            q = pltpu.roll(r[n:, 2 * zb * i:2 * zb * (i + 1)], zb, 1)
            dst[k + i] = p + jnp.where(lo, sign * q, -sign * q)

    def yfwd(c, k, kc):
        blk = ai.at[pl.ds(k, kc)]
        local(blk, blk, ra.at[c]).wait()
        ydft(ai, yf, k, kc, None, 1.0)
        for d in range(1, nb):
            t = lax.rem(b + d, nb)
            pltpu.make_async_remote_copy(
                yf.at[pl.ds(k, kc), pl.ds(t * zb, zb)], bi.at[pl.ds(k, kc), :, pl.ds(b * 2 * zb, 2 * zb)],
                ssem.at[1], rb.at[c], device_id=(t, a), device_id_type=MESH).start()
        local(yf.at[pl.ds(k, kc), pl.ds(b * zb, zb)], bi.at[pl.ds(k, kc), :, pl.ds(b * 2 * zb, 2 * zb)], rb.at[c]).start()

    chunks(yfwd)
    loads[2].wait()
    loads[3].wait()

    def zfilt(c, k, kc):
        blk = bi.at[pl.ds(k, kc)]
        local(blk, blk, rb.at[c]).wait()
        x = bi[pl.ds(k, kc)].reshape(kc * zb, 2 * n)
        f = _dot(x, tz[...])
        gg = g[pl.ds(k, kc)].reshape(kc * zb, n)
        v = f * jnp.concatenate([gg, gg], axis=1) * (1.0 / n)
        o = _dot(v, tz[...], ((1,), (1,)))
        bo[pl.ds(k, kc)] = o.reshape(kc, zb, 2 * n)
        for d in range(1, nb):
            t = lax.rem(b + d, nb)
            pltpu.make_async_remote_copy(
                bo.at[pl.ds(k, kc), :, pl.ds(t * 2 * zb, 2 * zb)], vi.at[pl.ds(k, kc), pl.ds(b * zb, zb)],
                ssem.at[2], rbo.at[c], device_id=(t, a), device_id_type=MESH).start()
        local(bo.at[pl.ds(k, kc), :, pl.ds(b * 2 * zb, 2 * zb)], vi.at[pl.ds(k, kc), pl.ds(b * zb, zb)], rbo.at[c]).start()

    chunks(zfilt)

    def yinv(c, k, kc):
        blk = vi.at[pl.ds(k, kc)]
        local(blk, blk, rbo.at[c]).wait()
        ydft(vi, iy, k, kc, 1.0 / n, -1.0)
        for d in range(1, na):
            t = lax.rem(a + d, na)
            pltpu.make_async_remote_copy(
                iy.at[pl.ds(k, kc), pl.ds(t * ya, ya)], ao.at[pl.ds(a * kl + k, kc)],
                ssem.at[3], rao.at[c], device_id=(b, t), device_id_type=MESH).start()
        local(iy.at[pl.ds(k, kc), pl.ds(a * ya, ya)], ao.at[pl.ds(a * kl + k, kc)], rao.at[c]).start()

    chunks(yinv)
    loads[4].wait()

    def wait_ao(c, k, kc):
        blk = ao.at[pl.ds(0, na * kc)]
        local(blk, blk, rao.at[c]).wait()

    chunks(wait_ao)

    def xinv(j, _):
        lo = lanes((kx, 2 * zb))
        parts = []
        for h in range(2):
            y = 4 * j + 2 * h
            p = ao2[pl.ds(y, kx, stride=ya), :]
            q = ao2[pl.ds(y + 1, kx, stride=ya), :]
            re = jnp.where(lo, p, pltpu.roll(q, zb, 1))
            im = jnp.where(lo, pltpu.roll(p, zb, 1), q)
            parts.append(jnp.concatenate([re, im], axis=0))
        d = jnp.concatenate(parts, axis=1)
        at = pl.ds(pl.multiple_of(j * rows, rows), rows)
        w[at, :] = _dot(d, txi[...], ((0,), (0,)))
        local(w.at[at], w_hbm.at[at], wsem).start()
        return 0

    lax.fori_loop(0, nj, xinv, 0)
    local(w, w_hbm, wsem).wait()
    sa = xs.at[pl.ds(0, (na - 1) * kl)]
    sb = yf.at[:, pl.ds(0, (nb - 1) * zb)]
    local(sa, sa, ssem.at[0]).wait()
    local(sb, sb, ssem.at[1]).wait()
    local(sb, sb, ssem.at[2]).wait()
    local(sa, sa, ssem.at[3]).wait()


def solution(mesh):
    na, nb = mesh.shape["a"], mesh.shape["b"]

    def body(u, g):
        n, ya, zb = u.shape
        kl = g.shape[0]
        kx = kl * na
        tabs = _tables(n, kx, nb)
        ut = jnp.transpose(u, (1, 2, 0)).reshape(ya * zb, n)
        nchunk = -(-kl // KC)
        nj = ya // 4
        vm = lambda *s: pltpu.VMEM(s, F32)
        dma = lambda *s: pltpu.SemaphoreType.DMA(s)
        hbm = pl.BlockSpec(memory_space=pl.ANY)
        w = pl.pallas_call(
            functools.partial(_kernel, n, na, nb, kl),
            name="fftfilter",
            out_shape=jax.ShapeDtypeStruct((ya * zb, n), F32),
            in_specs=[hbm] * 6,
            out_specs=hbm,
            scratch_shapes=[
                vm(ya * zb, n), vm(kl, zb, n), vm(*tabs[0].shape), vm(*tabs[1].shape), vm(*tabs[2].shape), vm(*tabs[3].shape),
                vm(kx, ya, 2 * zb), vm(kl, n, 2 * zb), vm(kl, n, 2 * zb), vm(kl, zb, 2 * n), vm(kl, zb, 2 * n),
                vm(kl, n, 2 * zb), vm(kl, n, 2 * zb), vm(kx, ya, 2 * zb), vm(ya * zb, n),
                dma(5), dma(nj), pltpu.SemaphoreType.DMA, dma(4), dma(nchunk), dma(nchunk), dma(nchunk), dma(nchunk),
            ],
            compiler_params=pltpu.CompilerParams(
                collective_id=0, has_side_effects=True, vmem_limit_bytes=60000 * 1024),
        )(ut, g, *[jnp.asarray(t) for t in tabs])
        return jnp.transpose(w.reshape(ya, zb, n), (2, 0, 1))

    return jax.shard_map(body, mesh=mesh, in_specs=(P(None, "a", "b"), P("a", "b", None)),
                         out_specs=P(None, "a", "b"), check_vma=False)
```

time: 417 us -> 130 us (0.31); the launches traced: 410 us -> 129 us
  blocking collectives: 145 us -> 0 us
  local copies, waits for them, and re-layouts: 141 us -> 3.13 us
  Pallas kernels: 0 us -> 126 us
  matrix products: 46.9 us -> 0 us
  other arithmetic: 44.3 us -> 0 us
  waiting for transfers between devices: 27.9 us -> 0 us
  starting transfers between devices: 4.56 us -> 0 us
    all_to_all x3 -> x0, blocking collectives: 145 us -> none  [the longest x1 56.5 us: local(): x = lax.all_to_all(x, 'b', 2, 3, tiled=True)]
    pallas_call x0 -> x1, Pallas kernels: none -> 126 us  [body(): pl.pallas_call(functools.partial(_kernel, n, na, nb, kl), name='fftfilter...]
    unnamed x22 -> x1, local copies, waits for them, and re-layouts: 58.2 us -> 3.13 us
    all_to_all x4 -> x0, other arithmetic: 36.3 us -> none  [the longest x1 9.15 us: local(): x = lax.all_to_all(x, 'b', 2, 3, tiled=True)]
    another operation x6 -> x0, local copies, waits for them, and re-layouts: 31.7 us -> none  [the longest x3 21.2 us: _line(): jnp.stack([e(x[0], c) + sign * e(x[1], s), e(x[1], c) - sign * e(x[0], s)])]
    dot_general x12 -> x0, matrix products: 28.5 us -> none  [the longest x4 10.8 us: _mm(): return jnp.dot(p, q, precision=HI, preferred_element_type=jnp.float32)]
    all_to_all x1 -> x0, waiting for transfers between devices: 27.9 us -> none  [local(): x = lax.all_to_all(x, 'a', 2, 1, tiled=True)]
    unnamed x8 -> x0, matrix products: 18.4 us -> none
  transfers between devices with their start and end apart: 1 -> 0, of which waited for: 1 -> 0; matrix products, arithmetic and copies ran while one was open for 0% -> 0% of each run, Pallas kernels for 0% -> 0%
where the time goes in v1:
time: 130 us; the launch traced here: 129 us
  Pallas kernels  126 us (97%)
  local copies, waits for them, and re-layouts  3.13 us (2%)
    pallas_call x1, Pallas kernels, body(): pl.pallas_call(functools.partial(_kernel, n, na, nb, kl), name='fftfilter...  126 us
    unnamed x1, local copies, waits for them, and re-layouts  3.13 us

profile of v1, /device:TPU:0, one launch (start us, length us, event | category | flops | bytes accessed | tf_op | source)
XLA Modules:
  0.0 129.2 jit_solution(1416449979932936044)
XLA Ops:
  0.0 126.0 %fftfilter.1 = f32[2048,256]{1,0:T(8,128)} custom-call(f32[2048,256]{1,0:T(8,128)} %bitcast.7, f32[17,64,256]{2,1,0:T(8,128)} %g_hbm.1, f32[272,256]{1,0:T(8,128)} %constant.8.clone.tx_hbm, f32[272,256]{1,0:T(8,128)} %constant.9.clone.txi_hbm, f32[512,256]{1,0:T(8,128)} %constant.10.clone.ty_hbm, f32[512,512]{1,0:T(8,128)} %constant.11.clone.tz_hbm), custom_call_target="tpu_custom_call" | custom-call | tf_op jit(solution)/shard_map/fftfilter/pallas_call | solution.py:221
  126.1 3.1 %copy.8 = f32[256,32,64]{0,2,1:T(8,128)} copy(f32[256,32,64]{0,2,1:T(8,128)} %bitcast.6) | data formatting | bytes 4194304

commit v2 on v1

v2 whole, which is shorter than its diff:
```python
import functools
import math
import numpy as np
import jax
import jax.numpy as jnp
from jax import lax
from jax.experimental import pallas as pl
from jax.experimental.pallas import tpu as pltpu
from jax.sharding import PartitionSpec as P

HI = lax.Precision.HIGHEST
MESH = pl.DeviceIdType.MESH
F32 = jnp.float32
KC = 2
GC = 2
LZ = 2
LY = 4
TX = 5
PX = 2
NP = 4


def _trig(n, rows, cols):
    r = np.arange(rows)[:, None]
    c = np.arange(cols)[None, :]
    ang = ((r * c) % n).astype(np.float32) * np.float32(2.0 * math.pi / n)
    ang = ang.astype(np.float64)
    return np.cos(ang).astype(np.float32), np.sin(ang).astype(np.float32)


def _plan(n, na, kl):
    modes = n // 2 + 1
    slots = kl - 1
    own = modes - kl * (na - 1)
    assert own + na - 2 == slots and slots % KC == 0
    kx = kl * np.arange(na)[:, None] + np.arange(slots)[None, :]
    kx[na - 1, own:] = kl * np.arange(na - 2) + slots
    return kx, kl * (na - 2) + slots, own


def _tables(n, na, nb, kl):
    kx, extra, _ = _plan(n, na, kl)
    pad = (-(kx.size + 1)) % 8
    c, s = _trig(n, n, n)

    def rows(t, k):
        return np.concatenate([t[k.reshape(-1)], t[[extra]], np.zeros((pad, n), np.float32)])

    tx = np.concatenate([rows(c, kx), rows(-s, kx)])
    wgt = np.where((np.arange(n) == 0) | (np.arange(n) == n // 2), 1.0, 2.0).astype(np.float32)[:, None] / np.float32(n)
    wc, ws = c * wgt, -s * wgt
    txi = []
    z7 = np.zeros((7, n), np.float32)
    for p, k in enumerate(range(0, kx.shape[1], KC * GC)):
        sel = kx[:, k:k + KC * GC].T.reshape(-1)
        txi += [wc[sel], ws[sel]]
        if p == PX:
            txi += [wc[[extra]], z7, ws[[extra]], z7]
    ty = np.concatenate([c, s], axis=0)
    zb = n // nb
    tz = []
    for b in range(nb):
        cb, sb = c[b * zb:(b + 1) * zb], s[b * zb:(b + 1) * zb]
        tz += [np.concatenate([cb, -sb], axis=1), np.concatenate([sb, cb], axis=1)]
    return [np.ascontiguousarray(t, dtype=np.float32) for t in (tx, np.concatenate(txi), ty, np.concatenate(tz))]


def _dot(p, q, dims=((1,), (0,))):
    return lax.dot_general(p, q, (dims, ((), ())), precision=HI, preferred_element_type=F32)


def _kernel(n, na, nb, kl, own, u_hbm, g_hbm, tx_hbm, txi_hbm, ty_hbm, tz_hbm, w_hbm,
            u, g, tx, txi, ty, tz, xs, ai, yf, bi, bo, vi, iy, ao, aox, w,
            lsem, usem, wsem, ssem, ra, rb, rbo, rao, rg):
    a, b = lax.axis_index("a"), lax.axis_index("b")
    ya, zb = n // na, n // nb
    slots = kl - 1
    nk = slots // KC
    kx = xs.shape[0]
    xrow = na * slots
    ex = na - 2
    rows = 4 * zb
    nj = ya * zb // rows
    lane = 2 * zb

    def local(src, dst, sem):
        return pltpu.make_async_copy(src, dst, sem)

    def remote(src, dst, s, r, t):
        return pltpu.make_async_remote_copy(src, dst, s, r, device_id=t, device_id_type=MESH)

    def wait(ref, sem):
        local(ref, ref, sem).wait()

    bar = pltpu.get_barrier_semaphore()
    for d in range(1, na):
        pl.semaphore_signal(bar, inc=1, device_id=(b, lax.rem(a + d, na)), device_id_type=MESH)
    for d in range(1, nb):
        pl.semaphore_signal(bar, inc=1, device_id=(lax.rem(b + d, nb), a), device_id_type=MESH)

    def load_u(j):
        at = pl.ds(pl.multiple_of(j * rows, rows), rows)
        return local(u_hbm.at[at], u.at[at], usem.at[j])

    loads = [local(s, d, lsem.at[i]) for i, (s, d) in enumerate(
        [(tx_hbm, tx), (ty_hbm, ty), (tz_hbm, tz), (txi_hbm, txi), (g_hbm.at[pl.ds(0, own)], g.at[pl.ds(0, own)])])]
    load_g = local(g_hbm.at[pl.ds(own, kl - own)], g.at[pl.ds(own, kl - own)], lsem.at[5])
    loads[0].start()
    for j in range(nj):
        load_u(j).start()
    for cp in loads[1:]:
        cp.start()

    @pl.when(a < na - 1)
    def _():
        load_g.start()

    def lanes(shape):
        return lax.broadcasted_iota(jnp.int32, shape, 1) < zb

    xs2 = xs.reshape(kx * ya, lane)

    def send_a(c, k, kc, y, yc):
        for d in range(1, na):
            t = lax.rem(a + d, na)
            remote(xs.at[pl.ds(t * slots + k, kc), pl.ds(y, yc)], ai.at[pl.ds(k, kc), pl.ds(a * ya + y, yc)],
                   ssem.at[0], ra.at[c], (b, t)).start()
        local(xs.at[pl.ds(a * slots + k, kc), pl.ds(y, yc)], ai.at[pl.ds(k, kc), pl.ds(a * ya + y, yc)], ra.at[c]).start()

    loads[0].wait()

    def xfwd(j, _):
        load_u(j).wait()
        r = _dot(tx[...], u[pl.ds(pl.multiple_of(j * rows, rows), rows), :], ((1,), (1,)))
        lo = lanes((kx, lane))
        for h in range(2):
            re = r[:kx, lane * h:lane * (h + 1)]
            im = r[kx:, lane * h:lane * (h + 1)]
            y = 4 * j + 2 * h
            xs2[pl.ds(y, kx, stride=ya), :] = jnp.where(lo, re, pltpu.roll(im, zb, 1))
            xs2[pl.ds(y + 1, kx, stride=ya), :] = jnp.where(lo, pltpu.roll(re, zb, 1), im)
        return 0

    lax.fori_loop(0, nj // 2, xfwd, 0)
    pl.semaphore_wait(bar, na + nb - 2)
    send_a(0, 0, KC, 0, ya // 2)
    lax.fori_loop(nj // 2, 3 * nj // 4, xfwd, 0)
    send_a(0, 0, KC, ya // 2, ya // 4)
    lax.fori_loop(3 * nj // 4, nj, xfwd, 0)
    send_a(0, 0, KC, 3 * ya // 4, ya // 4)

    def rest_a(c, _):
        send_a(c, c * KC, KC, 0, ya)
        return 0

    lax.fori_loop(1, nk, rest_a, 0)
    xsx, aix = xs.at[pl.ds(xrow, 1)], ai.at[pl.ds(slots, 1), pl.ds(a * ya, ya)]
    to_ex = remote(xsx, aix, ssem.at[4], ra.at[nk], (b, ex))
    to_me = local(xsx, aix, ra.at[nk])
    send_g = remote(g_hbm.at[slots], g.at[own + a], ssem.at[8], rg, (b, na - 1))

    @pl.when(a != ex)
    def _():
        to_ex.start()

    @pl.when(a == ex)
    def _():
        to_me.start()

    @pl.when(a < ex)
    def _():
        send_g.start()

    w[...] = jnp.zeros_like(w)
    aox[...] = jnp.zeros_like(aox)
    loads[1].wait()

    def ydft(src, dst, k, kc, scale, sign):
        x = jnp.concatenate([src[k + i] for i in range(kc)], axis=1)
        if scale is not None:
            x = x * scale
        r = _dot(ty[...], x)
        lo = lanes((n, lane))
        for i in range(kc):
            p = r[:n, lane * i:lane * (i + 1)]
            q = pltpu.roll(r[n:, lane * i:lane * (i + 1)], zb, 1)
            dst[k + i] = p + jnp.where(lo, sign * q, -sign * q)

    def yfwd(c, k, kc, s):
        wait(ai.at[pl.ds(k, kc)], ra.at[c])
        ydft(ai, yf, k, kc, None, 1.0)
        for d in range(1, nb):
            t = lax.rem(b + d, nb)
            remote(yf.at[pl.ds(k, kc), pl.ds(t * zb, zb)], bi.at[pl.ds(k, kc), :, pl.ds(b * lane, lane)],
                   s, rb.at[c], (t, a)).start()
        local(yf.at[pl.ds(k, kc), pl.ds(b * zb, zb)], bi.at[pl.ds(k, kc), :, pl.ds(b * lane, lane)], rb.at[c]).start()

    def zfilt(c, k, kc, s):
        wait(bi.at[pl.ds(k, kc)], rb.at[c])
        x = bi[pl.ds(k, kc)].reshape(kc * zb, 2 * n)
        f = _dot(x, tz[...])
        gg = g[pl.ds(k, kc)].reshape(kc * zb, n)
        v = f * jnp.concatenate([gg, gg], axis=1) * (1.0 / n)
        o = _dot(v, tz[...], ((1,), (1,)))
        bo[pl.ds(k, kc)] = o.reshape(kc, zb, 2 * n)
        for d in range(1, nb):
            t = lax.rem(b + d, nb)
            remote(bo.at[pl.ds(k, kc), :, pl.ds(t * lane, lane)], vi.at[pl.ds(k, kc), pl.ds(b * zb, zb)],
                   s, rbo.at[c if kc > 1 else nk - 1 + NP], (t, a)).start()
        local(bo.at[pl.ds(k, kc), :, pl.ds(b * lane, lane)], vi.at[pl.ds(k, kc), pl.ds(b * zb, zb)], rbo.at[c if kc > 1 else nk - 1 + NP]).start()

    def yinv(c, k, kc, s, pieces=1):
        wait(vi.at[pl.ds(k, kc)], rbo.at[c])
        ydft(vi, iy, k, kc, 1.0 / n, -1.0)
        yc = ya // pieces
        for p in range(pieces):
            dst = aox.at[pl.ds(0, 1)] if kc == 1 else ao.at[pl.ds(k, kc), a, pl.ds(p * yc, yc)]
            for d in range(1, na):
                t = lax.rem(a + d, na)
                remote(iy.at[pl.ds(k, kc), pl.ds(t * ya + p * yc, yc)], dst, s, rao.at[c + p], (b, t)).start()
            local(iy.at[pl.ds(k, kc), pl.ds(a * ya + p * yc, yc)], dst, rao.at[c + p]).start()

    ao2 = ao.reshape(slots * na * ya, lane)
    aox2 = aox.reshape(8 * ya, lane)
    m = GC * KC * na
    ly = 8

    def xinv(p, last):
        extra = p == PX
        trow = 2 * m * p + (16 if p > PX else 0)
        table = txi[trow:trow + 2 * m + (16 if extra else 0), :]
        srcs = [(ao2, p * m * ya, m)] + ([(aox2, 0, 8)] if extra else [])

        def body(j, _):
            if last:
                pc = j * ly // (ya // NP)

                @pl.when(j * ly % (ya // NP) == 0)
                def _():
                    wait(ao.at[pl.ds(0, KC), :, pl.ds(0, ya // NP)], rao.at[nk - 1 + pc])
            cols = []
            for h in range(ly // 2):
                parts = []
                for src, first, r in srcs:
                    lo = lanes((r, lane))
                    y = first + ly * j + 2 * h
                    f = src[pl.ds(y, r, stride=ya), :]
                    q = src[pl.ds(y + 1, r, stride=ya), :]
                    parts += [jnp.where(lo, f, pltpu.roll(q, zb, 1)), jnp.where(lo, pltpu.roll(f, zb, 1), q)]
                cols.append(jnp.concatenate(parts, axis=0))
            at = pl.ds(pl.multiple_of(j * (ly * zb), ly * zb), ly * zb)
            w[at, :] += _dot(jnp.concatenate(cols, axis=1), table, ((0,), (0,)))
            if last:
                local(w.at[at], w_hbm.at[at], wsem).start()
            return 0

        for c in range(GC * p, GC * (p + 1) - (1 if last else 0)):
            wait(ao.at[pl.ds(0, KC)], rao.at[c])
        if extra:
            wait(aox.at[0], rao.at[nk - 1 + NP])
        lax.fori_loop(0, ya // ly, body, 0)

    def step(t, _):
        @pl.when(t < nk)
        def _():
            yfwd(t, t * KC, KC, ssem.at[1])

        @pl.when((t == TX) & (a == ex))
        def _():
            yfwd(nk, slots, 1, ssem.at[5])

        @pl.when(t == LZ)
        def _():
            for i in (2, 4):
                loads[i].wait()

            @pl.when(a < na - 1)
            def _():
                load_g.wait()

        @pl.when((t == LZ + own // KC) & (a == na - 1))
        def _():
            wait(g.at[pl.ds(own, ex)], rg)

        @pl.when((t >= LZ) & (t < nk + LZ))
        def _():
            zfilt(t - LZ, (t - LZ) * KC, KC, ssem.at[2])

        @pl.when((t == TX + LZ) & (a == ex))
        def _():
            zfilt(nk, slots, 1, ssem.at[6])

        @pl.when(t >= LY)
        def _():
            yinv(t - LY, (t - LY) * KC, KC, ssem.at[3])

        @pl.when((t == TX + LY) & (a == ex))
        def _():
            yinv(nk - 1 + NP, slots, 1, ssem.at[7])

        for p in range(nk // GC - 2):
            @pl.when(t == GC * (p + 1) + LY)
            def _():
                if p == 0:
                    loads[3].wait()
                xinv(p, False)
        return 0

    lax.fori_loop(0, nk + LY - 1, step, 0)
    yinv(nk - 1, (nk - 1) * KC, KC, ssem.at[3], NP)
    xinv(nk // GC - 2, False)
    xinv(nk // GC - 1, True)
    wait_w = local(w, w_hbm, wsem)
    wait_w.wait()

    sa = xs.at[pl.ds(0, (na - 1) * slots)]
    sb = yf.at[pl.ds(0, slots), pl.ds(0, (nb - 1) * zb)]
    wait(sa, ssem.at[0])
    wait(sb, ssem.at[1])
    wait(sb, ssem.at[2])
    wait(sa, ssem.at[3])

    @pl.when(a != ex)
    def _():
        wait(xs.at[0], ssem.at[4])

    @pl.when(a == ex)
    def _():
        wait(yf.at[0, pl.ds(0, (nb - 1) * zb)], ssem.at[5])
        wait(yf.at[0, pl.ds(0, (nb - 1) * zb)], ssem.at[6])
        wait(xs.at[pl.ds(0, na - 1)], ssem.at[7])

    @pl.when(a < ex)
    def _():
        wait(g.at[0], ssem.at[8])


def solution(mesh):
    na, nb = mesh.shape["a"], mesh.shape["b"]

    def body(u, g):
        n, ya, zb = u.shape
        kl = g.shape[0]
        own = _plan(n, na, kl)[2]
        tabs = _tables(n, na, nb, kl)
        ut = jnp.transpose(u, (1, 2, 0)).reshape(ya * zb, n)
        nk = (kl - 1) // KC
        vm = lambda *s: pltpu.VMEM(s, F32)
        dma = lambda *s: pltpu.SemaphoreType.DMA(s)
        hbm = pl.BlockSpec(memory_space=pl.ANY)
        w = pl.pallas_call(
            functools.partial(_kernel, n, na, nb, kl, own),
            name="fftfilter",
            out_shape=jax.ShapeDtypeStruct((ya * zb, n), F32),
            in_specs=[hbm] * 6,
            out_specs=hbm,
            scratch_shapes=[
                vm(ya * zb, n), vm(kl, zb, n), *[vm(*t.shape) for t in tabs],
                vm(tabs[0].shape[0] // 2, ya, 2 * zb), vm(kl, n, 2 * zb), vm(kl, n, 2 * zb),
                vm(kl, zb, 2 * n), vm(kl, zb, 2 * n), vm(kl, n, 2 * zb), vm(kl, n, 2 * zb),
                vm(kl - 1, na, ya, 2 * zb), vm(8, ya, 2 * zb), vm(ya * zb, n),
                dma(6), dma(ya // 4), pltpu.SemaphoreType.DMA, dma(9),
                dma(nk + 1), dma(nk + 1), dma(nk + NP), dma(nk + NP), pltpu.SemaphoreType.DMA,
            ],
            compiler_params=pltpu.CompilerParams(
                collective_id=0, has_side_effects=True, vmem_limit_bytes=60000 * 1024),
        )(ut, g, *[jnp.asarray(t) for t in tabs])
        return jnp.transpose(w.reshape(ya, zb, n), (2, 0, 1))

    return jax.shard_map(body, mesh=mesh, in_specs=(P(None, "a", "b"), P("a", "b", None)),
                         out_specs=P(None, "a", "b"), check_vma=False)
```

time: 130 us -> 120 us (0.923)
  Pallas kernels: 126 us -> 117 us
    pallas_call x1, Pallas kernels: 126 us -> 117 us  [body(): pl.pallas_call(functools.partial(_kernel, n, na, nb, kl, own), name='fftf...]
where the time goes in v2:
time: 120 us
  Pallas kernels  117 us (98%)
  local copies, waits for them, and re-layouts  3.13 us (3%)
    pallas_call x1, Pallas kernels, body(): pl.pallas_call(functools.partial(_kernel, n, na, nb, kl, own), name='fftf...  117 us
    unnamed x1, local copies, waits for them, and re-layouts  3.13 us

profile of v2, /device:TPU:0, one launch (start us, length us, event | category | flops | bytes accessed | tf_op | source)
XLA Modules:
  0.0 120.2 jit_solution(13733313509001735352)
XLA Ops:
  0.0 117.1 %fftfilter.1 = f32[2048,256]{1,0:T(8,128)} custom-call(f32[2048,256]{1,0:T(8,128)} %bitcast.7, f32[17,64,256]{2,1,0:T(8,128)} %g_hbm.1, f32[272,256]{1,0:T(8,128)} %constant.8.clone.tx_hbm, f32[272,256]{1,0:T(8,128)} %constant.9.clone.txi_hbm, f32[512,256]{1,0:T(8,128)} %constant.10.clone.ty_hbm, f32[512,512]{1,0:T(8,128)} %constant.11.clone.tz_hbm), custom_call_target="tpu_custom_call" | custom-call | tf_op jit(solution)/shard_map/fftfilter/pallas_call | solution.py:351
  117.1 3.1 %copy.8 = f32[256,32,64]{0,2,1:T(8,128)} copy(f32[256,32,64]{0,2,1:T(8,128)} %bitcast.6) | data formatting | bytes 4194304

commit v3 on v2

--- a/solution.py
+++ b/solution.py
@@ -12,11 +12,11 @@
 MESH = pl.DeviceIdType.MESH
 F32 = jnp.float32
 KC = 2
-GC = 2
+GC = 4
 LZ = 2
 LY = 4
 TX = 5
-PX = 2
+PX = 1
 NP = 4
 
 
@@ -62,16 +62,18 @@
     for b in range(nb):
         cb, sb = c[b * zb:(b + 1) * zb], s[b * zb:(b + 1) * zb]
         tz += [np.concatenate([cb, -sb], axis=1), np.concatenate([sb, cb], axis=1)]
-    return [np.ascontiguousarray(t, dtype=np.float32) for t in (tx, np.concatenate(txi), ty, np.concatenate(tz))]
+    tz = np.concatenate(tz, axis=0)
+    return [np.ascontiguousarray(t, dtype=np.float32) for t in (tx, np.concatenate(txi), ty, tz[:, :n], tz[:, n:])]
 
 
 def _dot(p, q, dims=((1,), (0,))):
     return lax.dot_general(p, q, (dims, ((), ())), precision=HI, preferred_element_type=F32)
 
 
-def _kernel(n, na, nb, kl, own, u_hbm, g_hbm, tx_hbm, txi_hbm, ty_hbm, tz_hbm, w_hbm,
-            u, g, tx, txi, ty, tz, xs, ai, yf, bi, bo, vi, iy, ao, aox, w,
-            lsem, usem, wsem, ssem, ra, rb, rbo, rao, rg):
+def _kernel(n, na, nb, kl, own, u_hbm, g_hbm, tab_hbm, *refs):
+    out, refs = refs[:n // na // 8], refs[n // na // 8:]
+    (u, g, tx, txi, ty, tz, xs, ai, yf, bi, bo, vi, iy, ao, aox, w,
+            lsem, usem, ssem, ra, rb, rbo, rao, rg) = refs
     a, b = lax.axis_index("a"), lax.axis_index("b")
     ya, zb = n // na, n // nb
     slots = kl - 1
@@ -102,9 +104,12 @@
         at = pl.ds(pl.multiple_of(j * rows, rows), rows)
         return local(u_hbm.at[at], u.at[at], usem.at[j])
 
-    loads = [local(s, d, lsem.at[i]) for i, (s, d) in enumerate(
-        [(tx_hbm, tx), (ty_hbm, ty), (tz_hbm, tz), (txi_hbm, txi), (g_hbm.at[pl.ds(0, own)], g.at[pl.ds(0, own)])])]
-    load_g = local(g_hbm.at[pl.ds(own, kl - own)], g.at[pl.ds(own, kl - own)], lsem.at[5])
+    loads, at = [], 0
+    for d in (tx, txi, ty, tz.at[:, pl.ds(0, n)], tz.at[:, pl.ds(n, n)]):
+        loads.append(local(tab_hbm.at[pl.ds(at, d.shape[0])], d, lsem.at[len(loads)]))
+        at += d.shape[0]
+    loads.append(local(g_hbm.at[pl.ds(0, own)], g.at[pl.ds(0, own)], lsem.at[5]))
+    load_g = local(g_hbm.at[pl.ds(own, kl - own)], g.at[pl.ds(own, kl - own)], lsem.at[6])
     loads[0].start()
     for j in range(nj):
         load_u(j).start()
@@ -149,31 +154,10 @@
     lax.fori_loop(3 * nj // 4, nj, xfwd, 0)
     send_a(0, 0, KC, 3 * ya // 4, ya // 4)
 
-    def rest_a(c, _):
-        send_a(c, c * KC, KC, 0, ya)
-        return 0
-
-    lax.fori_loop(1, nk, rest_a, 0)
-    xsx, aix = xs.at[pl.ds(xrow, 1)], ai.at[pl.ds(slots, 1), pl.ds(a * ya, ya)]
-    to_ex = remote(xsx, aix, ssem.at[4], ra.at[nk], (b, ex))
-    to_me = local(xsx, aix, ra.at[nk])
-    send_g = remote(g_hbm.at[slots], g.at[own + a], ssem.at[8], rg, (b, na - 1))
-
-    @pl.when(a != ex)
-    def _():
-        to_ex.start()
-
-    @pl.when(a == ex)
-    def _():
-        to_me.start()
-
-    @pl.when(a < ex)
-    def _():
-        send_g.start()
-
+    send_a(1, KC, KC, 0, ya)
     w[...] = jnp.zeros_like(w)
     aox[...] = jnp.zeros_like(aox)
-    loads[1].wait()
+    loads[2].wait()
 
     def ydft(src, dst, k, kc, scale, sign):
         x = jnp.concatenate([src[k + i] for i in range(kc)], axis=1)
@@ -235,8 +219,7 @@
             if last:
                 pc = j * ly // (ya // NP)
 
-                @pl.when(j * ly % (ya // NP) == 0)
-                def _():
+                if j * ly % (ya // NP) == 0:
                     wait(ao.at[pl.ds(0, KC), :, pl.ds(0, ya // NP)], rao.at[nk - 1 + pc])
             cols = []
             for h in range(ly // 2):
@@ -248,30 +231,61 @@
                     q = src[pl.ds(y + 1, r, stride=ya), :]
                     parts += [jnp.where(lo, f, pltpu.roll(q, zb, 1)), jnp.where(lo, pltpu.roll(f, zb, 1), q)]
                 cols.append(jnp.concatenate(parts, axis=0))
-            at = pl.ds(pl.multiple_of(j * (ly * zb), ly * zb), ly * zb)
-            w[at, :] += _dot(jnp.concatenate(cols, axis=1), table, ((0,), (0,)))
+            part = _dot(jnp.concatenate(cols, axis=1), table, ((0,), (0,)))
             if last:
-                local(w.at[at], w_hbm.at[at], wsem).start()
+                out[j][...] = w[j * ly * zb:(j + 1) * ly * zb, :] + part
+                return 0
+            w[pl.ds(pl.multiple_of(j * (ly * zb), ly * zb), ly * zb), :] += part
             return 0
 
         for c in range(GC * p, GC * (p + 1) - (1 if last else 0)):
             wait(ao.at[pl.ds(0, KC)], rao.at[c])
         if extra:
             wait(aox.at[0], rao.at[nk - 1 + NP])
-        lax.fori_loop(0, ya // ly, body, 0)
+        if last:
+            for j in range(ya // ly):
+                body(j, 0)
+        else:
+            lax.fori_loop(0, ya // ly, body, 0)
+
+    def send_extra():
+        xsx, aix = xs.at[pl.ds(xrow, 1)], ai.at[pl.ds(slots, 1), pl.ds(a * ya, ya)]
+        to_ex = remote(xsx, aix, ssem.at[4], ra.at[nk], (b, ex))
+        to_me = local(xsx, aix, ra.at[nk])
+        send_g = remote(g_hbm.at[slots], g.at[own + a], ssem.at[8], rg, (b, na - 1))
+
+        @pl.when(a != ex)
+        def _():
+            to_ex.start()
+
+        @pl.when(a == ex)
+        def _():
+            to_me.start()
+
+        @pl.when(a < ex)
+        def _():
+            send_g.start()
 
     def step(t, _):
         @pl.when(t < nk)
         def _():
             yfwd(t, t * KC, KC, ssem.at[1])
 
+        @pl.when(t < nk - 2)
+        def _():
+            send_a(t + 2, (t + 2) * KC, KC, 0, ya)
+
+        @pl.when(t == 1)
+        def _():
+            send_extra()
+
         @pl.when((t == TX) & (a == ex))
         def _():
             yfwd(nk, slots, 1, ssem.at[5])
 
         @pl.when(t == LZ)
         def _():
-            for i in (2, 4):
+            for i in (3, 4, 5):
                 loads[i].wait()
 
             @pl.when(a < na - 1)
@@ -298,20 +312,17 @@
         def _():
             yinv(nk - 1 + NP, slots, 1, ssem.at[7])
 
-        for p in range(nk // GC - 2):
+        for p in range(nk // GC - 1):
             @pl.when(t == GC * (p + 1) + LY)
             def _():
                 if p == 0:
-                    loads[3].wait()
+                    loads[1].wait()
                 xinv(p, False)
         return 0
 
     lax.fori_loop(0, nk + LY - 1, step, 0)
     yinv(nk - 1, (nk - 1) * KC, KC, ssem.at[3], NP)
-    xinv(nk // GC - 2, False)
     xinv(nk // GC - 1, True)
-    wait_w = local(w, w_hbm, wsem)
-    wait_w.wait()
 
     sa = xs.at[pl.ds(0, (na - 1) * slots)]
     sb = yf.at[pl.ds(0, slots), pl.ds(0, (nb - 1) * zb)]
@@ -351,21 +362,21 @@
         w = pl.pallas_call(
             functools.partial(_kernel, n, na, nb, kl, own),
             name="fftfilter",
-            out_shape=jax.ShapeDtypeStruct((ya * zb, n), F32),
-            in_specs=[hbm] * 6,
-            out_specs=hbm,
+            out_shape=[jax.ShapeDtypeStruct((8 * zb, n), F32)] * (ya // 8),
+            in_specs=[hbm] * 3,
+            out_specs=[pl.BlockSpec(memory_space=pltpu.VMEM)] * (ya // 8),
             scratch_shapes=[
-                vm(ya * zb, n), vm(kl, zb, n), *[vm(*t.shape) for t in tabs],
+                vm(ya * zb, n), vm(kl, zb, n), *[vm(*t.shape) for t in tabs[:3]], vm(2 * n, 2 * n),
                 vm(tabs[0].shape[0] // 2, ya, 2 * zb), vm(kl, n, 2 * zb), vm(kl, n, 2 * zb),
                 vm(kl, zb, 2 * n), vm(kl, zb, 2 * n), vm(kl, n, 2 * zb), vm(kl, n, 2 * zb),
                 vm(kl - 1, na, ya, 2 * zb), vm(8, ya, 2 * zb), vm(ya * zb, n),
-                dma(6), dma(ya // 4), pltpu.SemaphoreType.DMA, dma(9),
+                dma(7), dma(ya // 4), dma(9),
                 dma(nk + 1), dma(nk + 1), dma(nk + NP), dma(nk + NP), pltpu.SemaphoreType.DMA,
             ],
             compiler_params=pltpu.CompilerParams(
-                collective_id=0, has_side_effects=True, vmem_limit_bytes=60000 * 1024),
-        )(ut, g, *[jnp.asarray(t) for t in tabs])
-        return jnp.transpose(w.reshape(ya, zb, n), (2, 0, 1))
+                collective_id=0, has_side_effects=True, vmem_limit_bytes=54000000),
+        )(ut, g, jnp.asarray(np.concatenate(tabs)))
+        return jnp.transpose(jnp.concatenate(w).reshape(ya, zb, n), (2, 0, 1))
 
     return jax.shard_map(body, mesh=mesh, in_specs=(P(None, "a", "b"), P("a", "b", None)),
                          out_specs=P(None, "a", "b"), check_vma=False)

time: 120 us -> 119 us (level)
  local copies, waits for them, and re-layouts: 3.13 us -> 0 us
  other arithmetic: 0 us -> 1.46 us
    unnamed x1 -> x0, local copies, waits for them, and re-layouts: 3.13 us -> none
    concatenate x0 -> x1, other arithmetic: none -> 1.46 us  [body(): return jnp.transpose(jnp.concatenate(w).reshape(ya, zb, n), (2, 0, 1))]
where the time goes in v3:
time: 119 us
  Pallas kernels  117 us (98%)
  other arithmetic  1.46 us (1%)
    pallas_call x1, Pallas kernels, body(): pl.pallas_call(functools.partial(_kernel, n, na, nb, kl, own), name='fftf...  117 us

profile of v3, /device:TPU:0, one launch (start us, length us, event | category | flops | bytes accessed | tf_op | source)
XLA Modules:
  0.0 118.7 jit_solution(18127737209298309039)
XLA Ops:
  0.0 117.2 %fftfilter.1 = (f32[512,256]{1,0:T(8,128)S(1)}, f32[512,256]{1,0:T(8,128)S(1)}, f32[512,256]{1,0:T(8,128)S(1)}, f32[512,256]{1,0:T(8,128)S(1)}) custom-call(f32[2048,256]{1,0:T(8,128)} %bitcast.6, f32[17,64,256]{2,1,0:T(8,128)} %g_hbm.1, f32[2080,256]{1,0:T(8,128)} %constant.2.clone.tab_hbm), custom_call_target="tpu_custom_call" | custom-call | tf_op jit(solution)/shard_map/fftfilter/pallas_call | solution.py:362
  117.2 1.5 %pad_maximum_fusion = f32[2048,256]{1,0:T(8,128)} fusion(f32[512,256]{1,0:T(8,128)S(1)} %get-tuple-element.12, f32[512,256]{1,0:T(8,128)S(1)} %get-tuple-element.11, f32[512,256]{1,0:T(8,128)S(1)} %get-tuple-element.10, f32[512,256]{1,0:T(8,128)S(1)} %get-tuple-element.9), kind=kLoop, calls=%fused_computation | loop fusion | flops 1572864 | bytes 4194304 | tf_op jit(solution)/shard_map/concatenate | solution.py:379

commit v4 on v3

v4 whole, which is shorter than its diff:
```python
import functools
import math
import numpy as np
import jax
import jax.numpy as jnp
from jax import lax
from jax.experimental import pallas as pl
from jax.experimental.pallas import tpu as pltpu
from jax.sharding import PartitionSpec as P

HI = lax.Precision.HIGHEST
MESH = pl.DeviceIdType.MESH
F32 = jnp.float32
KC = 2
LZ = 2
LY = 4
TX = 5
PASSES = (8, 12)


def _trig(n, rows, cols):
    r = np.arange(rows)[:, None]
    c = np.arange(cols)[None, :]
    ang = ((r * c) % n).astype(np.float32) * np.float32(2.0 * math.pi / n)
    ang = ang.astype(np.float64)
    return np.cos(ang).astype(np.float32), np.sin(ang).astype(np.float32)


def _plan(n, na, kl):
    modes = n // 2 + 1
    slots = kl - 1
    own = modes - kl * (na - 1)
    assert own + na - 2 == slots and slots % KC == 0
    kx = kl * np.arange(na)[:, None] + np.arange(slots)[None, :]
    kx[na - 1, own:] = kl * np.arange(na - 2) + slots
    return kx, kl * (na - 2) + slots, own


def _tables(n, na, nb, kl):
    kx, extra, _ = _plan(n, na, kl)
    c, s = _trig(n, n, n)

    def rows(t):
        last = np.zeros((na, n), np.float32)
        last[na - 2] = t[extra]
        return np.concatenate([t[kx.T.reshape(-1)], last])

    m = KC * na
    fc, fs = rows(c), rows(-s)
    tx = np.concatenate([fc[:m], fs[:m], fc[m:], fs[m:]])
    wgt = np.where((np.arange(n) == 0) | (np.arange(n) == n // 2), 1.0, 2.0).astype(np.float32)[:, None] / np.float32(n)
    wc, ws = c * wgt, -s * wgt
    wc, ws = rows(wc), rows(ws)
    txi = []
    for lo, hi in zip((0,) + PASSES, PASSES + (kl,)):
        txi += [wc[lo * na:hi * na], ws[lo * na:hi * na]]
    ty = np.concatenate([c, s], axis=0)
    zb = n // nb
    tz = []
    for b in range(nb):
        cb, sb = c[b * zb:(b + 1) * zb], s[b * zb:(b + 1) * zb]
        tz += [np.concatenate([cb, -sb], axis=1), np.concatenate([sb, cb], axis=1)]
    tz = np.concatenate(tz, axis=0)
    return [np.ascontiguousarray(t, dtype=np.float32) for t in (tx, np.concatenate(txi), ty, tz[:, :n], tz[:, n:])]


def _dot(p, q, dims=((1,), (0,))):
    return lax.dot_general(p, q, (dims, ((), ())), precision=HI, preferred_element_type=F32)


def _kernel(n, na, nb, kl, own, u_hbm, g_hbm, tab_hbm, *refs):
    out, refs = refs[:n // na // 8], refs[n // na // 8:]
    (u, g, tx, txi, ty, tz, xs, ai, yf, bi, bo, vi, iy, ao, w,
            lsem, usem, ssem, ra, rb, rbo, rao, rg) = refs
    a, b = lax.axis_index("a"), lax.axis_index("b")
    ya, zb = n // na, n // nb
    slots = kl - 1
    n2 = slots // KC - 1
    nk = n2 + KC
    ex = na - 2
    rows = 4 * zb
    nj = ya * zb // rows
    lane = 2 * zb

    def local(src, dst, sem):
        return pltpu.make_async_copy(src, dst, sem)

    def remote(src, dst, s, r, t):
        return pltpu.make_async_remote_copy(src, dst, s, r, device_id=t, device_id_type=MESH)

    def wait(ref, sem):
        local(ref, ref, sem).wait()

    bar = pltpu.get_barrier_semaphore()
    for d in range(1, na):
        pl.semaphore_signal(bar, inc=1, device_id=(b, lax.rem(a + d, na)), device_id_type=MESH)
    for d in range(1, nb):
        pl.semaphore_signal(bar, inc=1, device_id=(lax.rem(b + d, nb), a), device_id_type=MESH)

    def load_u(j):
        at = pl.ds(pl.multiple_of(j * rows, rows), rows)
        return local(u_hbm.at[at], u.at[at], usem.at[j])

    loads, at = [], 0
    for d in (tx, txi, ty, tz.at[:, pl.ds(0, n)], tz.at[:, pl.ds(n, n)]):
        loads.append(local(tab_hbm.at[pl.ds(at, d.shape[0])], d, lsem.at[len(loads)]))
        at += d.shape[0]
    loads.append(local(g_hbm.at[pl.ds(0, own)], g.at[pl.ds(0, own)], lsem.at[5]))
    load_g = local(g_hbm.at[pl.ds(own, kl - own)], g.at[pl.ds(own, kl - own)], lsem.at[6])
    loads[0].start()
    for j in range(nj):
        load_u(j).start()
    for cp in loads[1:]:
        cp.start()

    @pl.when(a < na - 1)
    def _():
        load_g.start()

    def lanes(shape):
        return lax.broadcasted_iota(jnp.int32, shape, 1) < zb

    xs2 = xs.reshape(kl * na * ya, lane)

    def send_a(c, k, kc):
        for d in range(1, na):
            t = lax.rem(a + d, na)
            remote(xs.at[pl.ds(k, kc), t], ai.at[pl.ds(k, kc), pl.ds(a * ya, ya)], ssem.at[0], ra.at[c], (b, t)).start()
        local(xs.at[pl.ds(k, kc), a], ai.at[pl.ds(k, kc), pl.ds(a * ya, ya)], ra.at[c]).start()

    def xfwd(r0, nr, first):
        lo = lanes((nr, lane))

        def body(j, _):
            if first:
                load_u(j).wait()
            r = _dot(tx[2 * r0:2 * (r0 + nr), :], u[pl.ds(pl.multiple_of(j * rows, rows), rows), :], ((1,), (1,)))
            for h in range(2):
                re = r[:nr, lane * h:lane * (h + 1)]
                im = r[nr:, lane * h:lane * (h + 1)]
                y = r0 * ya + 4 * j + 2 * h
                xs2[pl.ds(y, nr, stride=ya), :] = jnp.where(lo, re, pltpu.roll(im, zb, 1))
                xs2[pl.ds(y + 1, nr, stride=ya), :] = jnp.where(lo, pltpu.roll(re, zb, 1), im)
            return 0

        lax.fori_loop(0, nj, body, 0)

    loads[0].wait()
    xfwd(0, KC * na, True)
    pl.semaphore_wait(bar, na + nb - 2)
    send_a(0, 0, KC)
    xfwd(KC * na, (kl - KC) * na, False)
    send_a(1, KC, KC)
    ao[slots, 0:ex] = jnp.zeros((ex, ya, lane), F32)
    ao[slots, ex + 1:na] = jnp.zeros((na - ex - 1, ya, lane), F32)
    w[...] = jnp.zeros_like(w)
    loads[2].wait()

    def ydft(src, dst, k, kc, scale, sign):
        x = jnp.concatenate([src[k + i] for i in range(kc)], axis=1)
        if scale is not None:
            x = x * scale
        r = _dot(ty[...], x)
        lo = lanes((n, lane))
        for i in range(kc):
            p = r[:n, lane * i:lane * (i + 1)]
            q = pltpu.roll(r[n:, lane * i:lane * (i + 1)], zb, 1)
            dst[k + i] = p + jnp.where(lo, sign * q, -sign * q)

    def yfwd(c, k, kc, s):
        wait(ai.at[pl.ds(k, kc)], ra.at[c])
        ydft(ai, yf, k, kc, None, 1.0)
        for d in range(1, nb):
            t = lax.rem(b + d, nb)
            remote(yf.at[pl.ds(k, kc), pl.ds(t * zb, zb)], bi.at[pl.ds(k, kc), :, pl.ds(b * lane, lane)],
                   s, rb.at[c], (t, a)).start()
        local(yf.at[pl.ds(k, kc), pl.ds(b * zb, zb)], bi.at[pl.ds(k, kc), :, pl.ds(b * lane, lane)], rb.at[c]).start()

    def zfilt(c, k, kc, s):
        wait(bi.at[pl.ds(k, kc)], rb.at[c])
        x = bi[pl.ds(k, kc)].reshape(kc * zb, 2 * n)
        f = _dot(x, tz[...])
        gg = g[pl.ds(k, kc)].reshape(kc * zb, n)
        v = f * jnp.concatenate([gg, gg], axis=1) * (1.0 / n)
        o = _dot(v, tz[...], ((1,), (1,)))
        bo[pl.ds(k, kc)] = o.reshape(kc, zb, 2 * n)
        for d in range(1, nb):
            t = lax.rem(b + d, nb)
            remote(bo.at[pl.ds(k, kc), :, pl.ds(t * lane, lane)], vi.at[pl.ds(k, kc), pl.ds(b * zb, zb)],
                   s, rbo.at[c], (t, a)).start()
        local(bo.at[pl.ds(k, kc), :, pl.ds(b * lane, lane)], vi.at[pl.ds(k, kc), pl.ds(b * zb, zb)], rbo.at[c]).start()

    def yinv(c, k, kc, s):
        wait(vi.at[pl.ds(k, kc)], rbo.at[c])
        ydft(vi, iy, k, kc, 1.0 / n, -1.0)
        for d in range(1, na):
            t = lax.rem(a + d, na)
            remote(iy.at[pl.ds(k, kc), pl.ds(t * ya, ya)], ao.at[pl.ds(k, kc), a], s, rao.at[c], (b, t)).start()
        local(iy.at[pl.ds(k, kc), pl.ds(a * ya, ya)], ao.at[pl.ds(k, kc), a], rao.at[c]).start()

    ao2 = ao.reshape(kl * na * ya, lane)
    ly = 8

    def xinv(k0, k1, last):
        m = (k1 - k0) * na
        lo = lanes((m, lane))
        table = txi[2 * k0 * na:2 * k1 * na, :]

        def body(j, _):
            cols = []
            for h in range(ly // 2):
                y = k0 * na * ya + ly * j + 2 * h
                p = ao2[pl.ds(y, m, stride=ya), :]
                q = ao2[pl.ds(y + 1, m, stride=ya), :]
                cols.append(jnp.concatenate(
                    [jnp.where(lo, p, pltpu.roll(q, zb, 1)), jnp.where(lo, pltpu.roll(p, zb, 1), q)], axis=0))
            part = _dot(jnp.concatenate(cols, axis=1), table, ((0,), (0,)))
            if last:
                out[j][...] = w[j * ly * zb:(j + 1) * ly * zb, :] + part
                return 0
            w[pl.ds(pl.multiple_of(j * (ly * zb), ly * zb), ly * zb), :] += part
            return 0

        for k in range(k0, k1):
            if k < KC * n2:
                if k % KC == 0:
                    wait(ao.at[pl.ds(0, KC)], rao.at[k // KC])
            elif k < slots:
                wait(ao.at[0], rao.at[k - n2])
            else:
                wait(ao.at[0, 0], rao.at[k - n2])
        if last:
            for j in range(ya // ly):
                body(j, 0)
        else:
            lax.fori_loop(0, ya // ly, body, 0)

    def send_extra():
        xsx, aix = xs.at[pl.ds(slots, 1), ex], ai.at[pl.ds(slots, 1), pl.ds(a * ya, ya)]
        to_ex = remote(xsx, aix, ssem.at[4], ra.at[nk], (b, ex))
        to_me = local(xsx, aix, ra.at[nk])
        send_g = remote(g_hbm.at[slots], g.at[own + a], ssem.at[8], rg, (b, na - 1))

        @pl.when(a != ex)
        def _():
            to_ex.start()

        @pl.when(a == ex)
        def _():
            to_me.start()

        @pl.when(a < ex)
        def _():
            send_g.start()

    def stage(f, t, sem, sem_extra):
        @pl.when((t >= 0) & (t < n2))
        def _():
            f(t, t * KC, KC, ssem.at[sem])

        extra = (t == TX) & (a == ex)

        @pl.when(((t >= n2) & (t < nk)) | extra)
        def _():
            k = jnp.where(t == TX, slots, t + n2 * (KC - 1))
            f(k - n2 * (KC - 1), k, 1, ssem.at[jnp.where(t == TX, sem_extra, sem)])

    def step(t, _):
        stage(yfwd, t, 1, 5)

        @pl.when(t + 2 < n2)
        def _():
            send_a(t + 2, (t + 2) * KC, KC)

        @pl.when((t + 2 >= n2) & (t + 2 < nk))
        def _():
            send_a(t + 2, t + 2 + n2 * (KC - 1), 1)

        @pl.when(t == 1)
        def _():
            send_extra()

        @pl.when(t == LZ)
        def _():
            for i in (3, 4, 5):
                loads[i].wait()

            @pl.when(a < na - 1)
            def _():
                load_g.wait()

        @pl.when((t == LZ + own // KC) & (a == na - 1))
        def _():
            wait(g.at[pl.ds(own, ex)], rg)

        stage(zfilt, t - LZ, 2, 6)
        stage(yinv, t - LY, 3, 7)

        @pl.when(t == PASSES[0] // KC + LY)
        def _():
            loads[1].wait()
            xinv(0, PASSES[0], False)
        return 0

    lax.fori_loop(0, nk + LY, step, 0)
    for k0, k1 in zip(PASSES, PASSES[1:] + (kl,)):
        xinv(k0, k1, k1 == kl)

    sa = xs.at[pl.ds(0, slots), pl.ds(0, na - 1)]
    sb = yf.at[pl.ds(0, slots), pl.ds(0, (nb - 1) * zb)]
    wait(sa, ssem.at[0])
    wait(sb, ssem.at[1])
    wait(sb, ssem.at[2])
    wait(sa, ssem.at[3])

    @pl.when(a != ex)
    def _():
        wait(xs.at[0, 0], ssem.at[4])

    @pl.when(a == ex)
    def _():
        wait(yf.at[0, pl.ds(0, (nb - 1) * zb)], ssem.at[5])
        wait(yf.at[0, pl.ds(0, (nb - 1) * zb)], ssem.at[6])
        wait(xs.at[0, pl.ds(0, na - 1)], ssem.at[7])

    @pl.when(a < ex)
    def _():
        wait(g.at[0], ssem.at[8])


def solution(mesh):
    na, nb = mesh.shape["a"], mesh.shape["b"]

    def body(u, g):
        n, ya, zb = u.shape
        kl = g.shape[0]
        own = _plan(n, na, kl)[2]
        tabs = _tables(n, na, nb, kl)
        ut = jnp.transpose(u, (1, 2, 0)).reshape(ya * zb, n)
        nk = (kl - 1) // KC + KC
        vm = lambda *s: pltpu.VMEM(s, F32)
        dma = lambda *s: pltpu.SemaphoreType.DMA(s)
        hbm = pl.BlockSpec(memory_space=pl.ANY)
        w = pl.pallas_call(
            functools.partial(_kernel, n, na, nb, kl, own),
            name="fftfilter",
            out_shape=[jax.ShapeDtypeStruct((8 * zb, n), F32)] * (ya // 8),
            in_specs=[hbm] * 3,
            out_specs=[pl.BlockSpec(memory_space=pltpu.VMEM)] * (ya // 8),
            scratch_shapes=[
                vm(ya * zb, n), vm(kl, zb, n), *[vm(*t.shape) for t in tabs[:3]], vm(2 * n, 2 * n),
                vm(kl, na, ya, 2 * zb), vm(kl, n, 2 * zb), vm(kl, n, 2 * zb),
                vm(kl, zb, 2 * n), vm(kl, zb, 2 * n), vm(kl, n, 2 * zb), vm(kl, n, 2 * zb),
                vm(kl, na, ya, 2 * zb), vm(ya * zb, n),
                dma(7), dma(ya // 4), dma(9),
                dma(nk), dma(nk), dma(nk), dma(nk), pltpu.SemaphoreType.DMA,
            ],
            compiler_params=pltpu.CompilerParams(
                collective_id=0, has_side_effects=True, vmem_limit_bytes=54000000),
        )(ut, g, jnp.asarray(np.concatenate(tabs)))
        return jnp.transpose(jnp.concatenate(w).reshape(ya, zb, n), (2, 0, 1))

    return jax.shard_map(body, mesh=mesh, in_specs=(P(None, "a", "b"), P("a", "b", None)),
                         out_specs=P(None, "a", "b"), check_vma=False)
```

time: 119 us -> 119 us (level)
  no operation moved by 1% of the time
where the time goes in v4:
time: 119 us
  Pallas kernels  118 us (99%)
  other arithmetic  1.46 us (1%)
    pallas_call x1, Pallas kernels, body(): pl.pallas_call(functools.partial(_kernel, n, na, nb, kl, own), name='fftf...  118 us

profile of v4, /device:TPU:0, one launch (start us, length us, event | category | flops | bytes accessed | tf_op | source)
XLA Modules:
  0.0 119.2 jit_solution(9033617037973882462)
XLA Ops:
  0.0 117.8 %fftfilter.1 = (f32[512,256]{1,0:T(8,128)S(1)}, f32[512,256]{1,0:T(8,128)S(1)}, f32[512,256]{1,0:T(8,128)S(1)}, f32[512,256]{1,0:T(8,128)S(1)}) custom-call(f32[2048,256]{1,0:T(8,128)} %bitcast.6, f32[17,64,256]{2,1,0:T(8,128)} %g_hbm.1, f32[2080,256]{1,0:T(8,128)} %constant.2.clone.tab_hbm), custom_call_target="tpu_custom_call" | custom-call | tf_op jit(solution)/shard_map/fftfilter/pallas_call | solution.py:344
  117.8 1.5 %pad_maximum_fusion = f32[2048,256]{1,0:T(8,128)} fusion(f32[512,256]{1,0:T(8,128)S(1)} %get-tuple-element.12, f32[512,256]{1,0:T(8,128)S(1)} %get-tuple-element.11, f32[512,256]{1,0:T(8,128)S(1)} %get-tuple-element.10, f32[512,256]{1,0:T(8,128)S(1)} %get-tuple-element.9), kind=kLoop, calls=%fused_computation | loop fusion | flops 1572864 | bytes 4194304 | tf_op jit(solution)/shard_map/concatenate | solution.py:361

commit v5 on v4

--- a/solution.py
+++ b/solution.py
@@ -15,6 +15,7 @@
 LZ = 2
 LY = 4
 TX = 5
+XCUT = 8
 PASSES = (8, 12)
 
 
@@ -47,7 +48,8 @@
 
     m = KC * na
     fc, fs = rows(c), rows(-s)
-    tx = np.concatenate([fc[:m], fs[:m], fc[m:], fs[m:]])
+    cut = XCUT * na
+    tx = np.concatenate([fc[:m], fs[:m], fc[m:cut], fs[m:cut], fc[cut:], fs[cut:]])
     wgt = np.where((np.arange(n) == 0) | (np.arange(n) == n // 2), 1.0, 2.0).astype(np.float32)[:, None] / np.float32(n)
     wc, ws = c * wgt, -s * wgt
     wc, ws = rows(wc), rows(ws)
@@ -149,11 +151,10 @@
     xfwd(0, KC * na, True)
     pl.semaphore_wait(bar, na + nb - 2)
     send_a(0, 0, KC)
-    xfwd(KC * na, (kl - KC) * na, False)
+    xfwd(KC * na, (XCUT - KC) * na, False)
     send_a(1, KC, KC)
     ao[slots, 0:ex] = jnp.zeros((ex, ya, lane), F32)
     ao[slots, ex + 1:na] = jnp.zeros((na - ex - 1, ya, lane), F32)
-    w[...] = jnp.zeros_like(w)
     loads[2].wait()
 
     def ydft(src, dst, k, kc, scale, sign):
@@ -302,7 +303,11 @@
             xinv(0, PASSES[0], False)
         return 0
 
-    lax.fori_loop(0, nk + LY, step, 0)
+    yfwd(0, 0, KC, ssem.at[1])
+    xfwd(XCUT * na, (kl - XCUT) * na, False)
+    send_a(2, 2 * KC, KC)
+    w[...] = jnp.zeros_like(w)
+    lax.fori_loop(1, nk + LY, step, 0)
     for k0, k1 in zip(PASSES, PASSES[1:] + (kl,)):
         xinv(k0, k1, k1 == kl)
 

time: 119 us -> 115 us (0.966)
  Pallas kernels: 118 us -> 114 us
    pallas_call x1, Pallas kernels: 118 us -> 114 us  [body(): pl.pallas_call(functools.partial(_kernel, n, na, nb, kl, own), name='fftf...]
where the time goes in v5:
time: 115 us
  Pallas kernels  114 us (99%)
  other arithmetic  1.46 us (1%)
    pallas_call x1, Pallas kernels, body(): pl.pallas_call(functools.partial(_kernel, n, na, nb, kl, own), name='fftf...  114 us

profile of v5, /device:TPU:0, one launch (start us, length us, event | category | flops | bytes accessed | tf_op | source)
XLA Modules:
  0.0 115.3 jit_solution(10442300613758972194)
XLA Ops:
  0.0 113.9 %fftfilter.1 = (f32[512,256]{1,0:T(8,128)S(1)}, f32[512,256]{1,0:T(8,128)S(1)}, f32[512,256]{1,0:T(8,128)S(1)}, f32[512,256]{1,0:T(8,128)S(1)}) custom-call(f32[2048,256]{1,0:T(8,128)} %bitcast.6, f32[17,64,256]{2,1,0:T(8,128)} %g_hbm.1, f32[2080,256]{1,0:T(8,128)} %constant.2.clone.tab_hbm), custom_call_target="tpu_custom_call" | custom-call | tf_op jit(solution)/shard_map/fftfilter/pallas_call | solution.py:349
  113.9 1.5 %pad_maximum_fusion = f32[2048,256]{1,0:T(8,128)} fusion(f32[512,256]{1,0:T(8,128)S(1)} %get-tuple-element.12, f32[512,256]{1,0:T(8,128)S(1)} %get-tuple-element.11, f32[512,256]{1,0:T(8,128)S(1)} %get-tuple-element.10, f32[512,256]{1,0:T(8,128)S(1)} %get-tuple-element.9), kind=kLoop, calls=%fused_computation | loop fusion | flops 1572864 | bytes 4194304 | tf_op jit(solution)/shard_map/concatenate | solution.py:366

commit v6 on v5

--- a/solution.py
+++ b/solution.py
@@ -269,13 +269,13 @@
     def step(t, _):
         stage(yfwd, t, 1, 5)
 
-        @pl.when(t + 2 < n2)
-        def _():
-            send_a(t + 2, (t + 2) * KC, KC)
-
-        @pl.when((t + 2 >= n2) & (t + 2 < nk))
-        def _():
-            send_a(t + 2, t + 2 + n2 * (KC - 1), 1)
+        @pl.when(t + 3 < n2)
+        def _():
+            send_a(t + 3, (t + 3) * KC, KC)
+
+        @pl.when((t + 3 >= n2) & (t + 3 < nk))
+        def _():
+            send_a(t + 3, t + 3 + n2 * (KC - 1), 1)
 
         @pl.when(t == 1)
         def _():
@@ -306,6 +306,7 @@
     yfwd(0, 0, KC, ssem.at[1])
     xfwd(XCUT * na, (kl - XCUT) * na, False)
     send_a(2, 2 * KC, KC)
+    send_a(3, 3 * KC, KC)
     w[...] = jnp.zeros_like(w)
     lax.fori_loop(1, nk + LY, step, 0)
     for k0, k1 in zip(PASSES, PASSES[1:] + (kl,)):

time: 115 us -> 115 us (level)
  no operation moved by 1% of the time
where the time goes in v6:
time: 115 us
  Pallas kernels  114 us (99%)
  other arithmetic  1.46 us (1%)
    pallas_call x1, Pallas kernels, body(): pl.pallas_call(functools.partial(_kernel, n, na, nb, kl, own), name='fftf...  114 us

profile of v6, /device:TPU:0, one launch (start us, length us, event | category | flops | bytes accessed | tf_op | source)
XLA Modules:
  0.0 115.3 jit_solution(11137302704871620245)
XLA Ops:
  0.0 113.8 %fftfilter.1 = (f32[512,256]{1,0:T(8,128)S(1)}, f32[512,256]{1,0:T(8,128)S(1)}, f32[512,256]{1,0:T(8,128)S(1)}, f32[512,256]{1,0:T(8,128)S(1)}) custom-call(f32[2048,256]{1,0:T(8,128)} %bitcast.6, f32[17,64,256]{2,1,0:T(8,128)} %g_hbm.1, f32[2080,256]{1,0:T(8,128)} %constant.2.clone.tab_hbm), custom_call_target="tpu_custom_call" | custom-call | tf_op jit(solution)/shard_map/fftfilter/pallas_call | solution.py:350
  113.9 1.5 %pad_maximum_fusion = f32[2048,256]{1,0:T(8,128)} fusion(f32[512,256]{1,0:T(8,128)S(1)} %get-tuple-element.12, f32[512,256]{1,0:T(8,128)S(1)} %get-tuple-element.11, f32[512,256]{1,0:T(8,128)S(1)} %get-tuple-element.10, f32[512,256]{1,0:T(8,128)S(1)} %get-tuple-element.9), kind=kLoop, calls=%fused_computation | loop fusion | flops 1572864 | bytes 4194304 | tf_op jit(solution)/shard_map/concatenate | solution.py:367
